TPU v7x, 32 devices: a whole 2x2x4 slice. The times are simulated.
32 devices in a mesh: row: 8 (over z, y), col: 4 (over x, core).
Axes of the slice: x: 2, y: 2, z: 4, core: 2. Of those that a mesh axis runs over, the one named last changes fastest.
Arguments:
- front: float32 [4096, 65536], P('row', 'col'), may hold values from -1 to 1
- omega: float32 [65536, 640], P(('col', 'row')), may hold values from -6 to 6
- leaf_pivots: int32 [16, 128], P('row'), may hold values from 0 to 255, as said below
- pivots_one: int32 [8, 128], P('row'), may hold values from 0 to 255, as said below
- pivots_two: int32 [4, 128], replicated, may hold values from 0 to 255, as said below
- pivots_three: int32 [2, 128], replicated, may hold values from 0 to 255, as said below
- pivots_four: int32 [1, 128], replicated, may hold values from 0 to 255, as said below
Outputs:
- samples: float32 [4096, 640], P('row')
- leaf_basis: float32 [16, 256, 128], P('row')
- basis_one: float32 [8, 256, 128], P('row')
- basis_two: float32 [8, 256, 128], P('row')
- basis_three: float32 [8, 256, 128], P('row')
- basis_four: float32 [8, 256, 128], P('row')
Inputs may be any that keep to these rules, and one draw needn't show every extreme that they name: `leaf_pivots`: each row holds 128 distinct indices. `pivots_one`: each row holds 128 distinct indices. `pivots_two`: each row holds 128 distinct indices. `pivots_three`: each row holds 128 distinct indices. `pivots_four`: each row holds 128 distinct indices.
All inputs are finite; a program needn't handle non-finite values.
Results may differ from a plain program's by a relative error of at most 0.0003.
Values sent between devices are 32-bit elements; how exact they have to be, the bound alone decides.
A program may use at most 128 MiB of HBM per device.

v0:
```python
import jax
import jax.numpy as jnp
from jax import lax
from jax.sharding import PartitionSpec as P

ridge = 1.0


def partner(block, axis, apart):
    count = lax.axis_size(axis)
    route = []
    for low in range(count):
        high = low | 1 << apart
        if high != low and high < count:
            route += [(low, high), (high, low)]
    return lax.ppermute(block, axis, route)


def interpolate(block, pivots):
    chosen = jnp.take(block, pivots, axis=0)
    gram = jnp.dot(
        chosen, chosen.T, precision=lax.Precision.HIGHEST, preferred_element_type=jnp.float32
    )
    gram = gram + ridge * jnp.eye(gram.shape[0], dtype=jnp.float32)
    cross = jnp.dot(
        block, chosen.T, precision=lax.Precision.HIGHEST, preferred_element_type=jnp.float32
    )
    factor = jnp.linalg.cholesky(gram)
    basis = jax.scipy.linalg.cho_solve((factor, True), cross.T).T
    return (basis, chosen)


def body(front, omega, leaf_pivots, pivots_one, pivots_two, pivots_three, pivots_four):
    rows_here = front.shape[0]
    width = omega.shape[1]
    partial_samples = jnp.dot(
        front,
        lax.all_gather(omega, "row", axis=0, tiled=True),
        precision=lax.Precision.HIGHEST,
        preferred_element_type=jnp.float32,
    )
    samples = lax.psum(partial_samples, "col")
    leaf_count = leaf_pivots.shape[0]
    leaf_size = rows_here // leaf_count
    blocks = samples.reshape(leaf_count, leaf_size, width)
    leaf_basis, skeleton = jax.vmap(interpolate)(blocks, leaf_pivots)
    merged = skeleton.reshape(leaf_size, width)
    basis_one, skeleton = interpolate(merged, pivots_one[0])
    position = lax.axis_index("row")
    upper_pivots = (pivots_two, pivots_three, pivots_four)
    results = []
    for level in range(3):
        other = partner(skeleton, "row", level)
        lower = position >> level & 1 == 0
        block = jnp.where(
            lower, jnp.concatenate([skeleton, other], 0), jnp.concatenate([other, skeleton], 0)
        )
        node = position >> level + 1
        chosen_pivots = lax.dynamic_index_in_dim(upper_pivots[level], node, 0, keepdims=False)
        basis, skeleton = interpolate(block, chosen_pivots)
        results.append(basis[None])
    return (samples, leaf_basis, basis_one[None], results[0], results[1], results[2])


def solution(mesh):
    in_specs = (
        P("row", "col"),
        P(("col", "row"), None),
        P("row", None),
        P("row", None),
        P(),
        P(),
        P(),
    )
    out_specs = (
        P("row", None),
        P("row", None, None),
        P("row", None, None),
        P("row", None, None),
        P("row", None, None),
        P("row", None, None),
    )
    return jax.shard_map(body, mesh=mesh, in_specs=in_specs, out_specs=out_specs, check_vma=False)
```

profile of v0, /device:TPU:0, one launch (start us, length us, event | category | flops | bytes accessed | tf_op | source)
XLA Modules:
  0.0 1109.0 jit_solution(16679894869034812231)
XLA Ops:
  8.3 1.2 compare_and_fusion.2
  13.2 794.1 %all-gather.2.cloned.1.call-done = f32[16384,640]{1,0:T(8,128)} async-done(((f32[2048,640]{1,0:T(8,128)}), f32[16384,640]{1,0:T(8,128)}) %all-gather.2.cloned.1.call-update) | async-done | bytes 41943056 | tf_op jit(solution)/shard_map/all_gather | solution.py:38
  807.3 87.6 %fusion.48 = f32[512,640]{1,0:T(8,128)} fusion(f32[512,16384]{1,0:T(8,128)} %param.12, f32[16384,640]{1,0:T(8,128)} %all-gather.2.cloned.1.call-done), kind=kOutput, calls=%fused_computation.107 | convolution fusion | flops 64424509440 | bytes 76808192 | tf_op jit(solution)/shard_map/dot_general | solution.py:36
  896.0 38.2 %all-reduce.2.cloned.1.call-done = f32[512,640]{1,0:T(8,128)} async-done(((f32[512,640]{1,0:T(8,128)}), f32[512,640]{1,0:T(8,128)}) %all-reduce.2.cloned.1.call-update) | async-done | bytes 1310736 | tf_op jit(solution)/shard_map/psum | solution.py:42
  934.1 2.8 gather_fusion
  937.1 0.8 gather_fusion.1
  938.0 1.5 collective-permute-start
  940.8 1.7 fusion.2
  942.5 2.2 fusion
  944.8 11.7 %cholesky.123 = f32[128,128]{1,0:T(8,128)S(1)} custom-call(f32[128,128]{1,0:T(8,128)S(1)} %fusion.40), custom_call_target="Cholesky" | custom-call | tf_op jit(solution)/shard_map/jit(cholesky)/cholesky | solution.py:28
  957.8 9.8 custom-call.25
  967.7 0.9 fusion.20
  968.6 23.6 %custom-call.18 = f32[2,128,128]{2,1,0:T(8,128)S(1)} custom-call(f32[2,128,128]{2,1,0:T(8,128)S(1)} %fusion.20), custom_call_target="Cholesky" | custom-call | tf_op jit(solution)/shard_map/vmap(jit(cholesky))/cholesky | solution.py:28
  992.4 0.8 select_bitcast_fusion
  993.2 19.7 %custom-call.19 = f32[2,1,128,128]{2,3,1,0:T(8,128)S(1)} custom-call(f32[2,1,128,128]{3,2,1,0:T(8,128)S(1)} %select_bitcast_fusion), custom_call_target="InvertDiagBlocksLowerTriangular" | custom-call | tf_op jit(solution)/shard_map/vmap(jit(_cho_solve))/triangular_solve | solution.py:29
  1014.1 0.8 copy.41
  1014.8 1.1 fusion.15
  1016.0 0.9 gather_fusion.2
  1017.6 1.5 collective-permute-start.1
  1020.5 11.7 %cholesky.134 = f32[128,128]{1,0:T(8,128)S(1)} custom-call(f32[128,128]{1,0:T(8,128)S(1)} %fusion.36), custom_call_target="Cholesky" | custom-call | tf_op jit(solution)/shard_map/jit(cholesky)/cholesky | solution.py:28
  1033.5 9.8 custom-call.26
  1043.9 0.8 copy.42
  1044.8 0.9 gather_fusion.3
  1045.8 2.5 collective-permute-start.2
  1049.6 11.9 %cholesky.145 = f32[128,128]{1,0:T(8,128)S(1)} custom-call(f32[128,128]{1,0:T(8,128)S(1)} %fusion.32), custom_call_target="Cholesky" | custom-call | tf_op jit(solution)/shard_map/jit(cholesky)/cholesky | solution.py:28
  1062.9 9.8 custom-call.27
  1074.1 0.9 gather_fusion.4
  1075.6 0.8 fusion.8
  1076.5 11.7 %cholesky.156 = f32[128,128]{1,0:T(8,128)S(1)} custom-call(f32[128,128]{1,0:T(8,128)S(1)} %fusion.28), custom_call_target="Cholesky" | custom-call | tf_op jit(solution)/shard_map/jit(cholesky)/cholesky | solution.py:28
  1089.6 9.8 custom-call.28
  1100.0 0.8 copy.44
  1100.7 1.1 copy.51
  (86 shorter events, 20.7 us)
Async XLA Ops:
  7.2 2.3 copy-start.4
  7.2 2.9 copy-start.5
  7.2 4.1 copy-start.6
  7.2 5.9 copy-start.3
  7.2 800.1 %all-gather.2.cloned.1.call-start = ((), (), s32[]{:S(2)}) async-start(), calls=%async_computation | async-start | bytes 47185920 | tf_op jit(solution)/shard_map/all_gather | solution.py:38
  7.9 926.2 %all-reduce.2.cloned.1.call-start = ((), (), s32[]{:S(2)}) async-start(), calls=%async_computation.1 | async-start | bytes 2621440 | tf_op jit(solution)/shard_map/psum | solution.py:42
  937.0 5.5 copy-start
  938.0 77.9 %collective-permute-start = (f32[128,640]{1,0:T(8,128)S(1)}, f32[128,640]{1,0:T(8,128)S(1)}, u32[]{:S(2)}, u32[]{:S(2)}) collective-permute-start(f32[128,640]{1,0:T(8,128)S(1)} %broadcast_select_fusion.3), channel_id=1, source_target_pairs={{0,4},{4,0},{8,12},{12,8},{16,20},{20,16},{24,28},{28,24},{1,5},{5... | collective-permute-start | bytes 983048 | tf_op jit(solution)/shard_map/ppermute | solution.py:16
  1016.0 29.8 %copy-start.2 = (pred[128]{0:T(512)(128)(4,1)S(1)}, pred[128]{0:T(512)(128)(4,1)}, u32[]{:S(2)}) copy-start(pred[128]{0:T(512)(128)(4,1)} %get-tuple-element.21) | copy-start | bytes 388
  1017.6 27.1 %collective-permute-start.1 = (f32[128,640]{1,0:T(8,128)S(1)}, f32[128,640]{1,0:T(8,128)S(1)}, u32[]{:S(2)}, u32[]{:S(2)}) collective-permute-start(f32[128,640]{1,0:T(8,128)S(1)} %broadcast_select_fusion.2), channel_id=1, source_target_pairs={{0,8},{8,0},{4,12},{12,4},{16,24},{24,16},{20,28},{28,20},{1,9},{9... | collective-permute-start | bytes 983048 | tf_op jit(solution)/shard_map/ppermute | solution.py:16
  1044.8 30.3 %copy-start.1 = (pred[128]{0:T(512)(128)(4,1)S(1)}, pred[128]{0:T(512)(128)(4,1)}, u32[]{:S(2)}) copy-start(pred[128]{0:T(512)(128)(4,1)} %compare_and_fusion) | copy-start | bytes 388
  1045.8 28.2 %collective-permute-start.2 = (f32[128,640]{1,0:T(8,128)S(1)}, f32[128,640]{1,0:T(8,128)S(1)}, u32[]{:S(2)}, u32[]{:S(2)}) collective-permute-start(f32[128,640]{1,0:T(8,128)S(1)} %broadcast_select_fusion.1), channel_id=1, source_target_pairs={{0,16},{16,0},{4,20},{20,4},{8,24},{24,8},{12,28},{28,12},{1,17},{... | collective-permute-start | bytes 983048 | tf_op jit(solution)/shard_map/ppermute | solution.py:16
Sparse Core Ops, SparseCore 0:
  9.6 797.6 all-gather.1
  895.0 39.0 all-reduce.1
where the time goes:
time: 1110 us
  waiting for transfers between devices  833 us (75%)
  other arithmetic  144 us (13%)
  matrix products  100 us (9%)
  between operations  14.9 us (1%)
  local copies, waits for them, and re-layouts  11.2 us (1%)
    all_gather x1, waiting for transfers between devices, body(): lax.all_gather(omega, 'row', axis=0, tiled=True)  794 us
    dot_general x1, matrix products, body(): jnp.dot(front, lax.all_gather(omega, 'row', axis=0, tiled=True), precisio...  87.6 us
    another operation x16, other arithmetic, interpolate(): factor = jnp.linalg.cholesky(gram)  73.6 us
    another operation x11, other arithmetic, interpolate(): basis = jax.scipy.linalg.cho_solve((factor, True), cross.T).T  63 us
    psum x1, waiting for transfers between devices, body(): samples = lax.psum(partial_samples, 'col')  38.2 us
  transfers between devices with their start and end apart: 5, of which 2 were waited for; matrix products, arithmetic and copies ran while one was open for 12% of the time, Pallas kernels for 0%

commit v1 on v0

v1 whole, which is shorter than its diff:
```python
import functools

import jax
import jax.numpy as jnp
from jax import lax
from jax.experimental import pallas as pl
from jax.experimental.pallas import tpu as pltpu
from jax.sharding import PartitionSpec as P

ridge = 1.0
MESH = pl.DeviceIdType.MESH
HIGHEST = lax.Precision.HIGHEST


def gather_matmul_kernel(
    n, depth, pieces, front_ref, omega_ref, out_ref, held, cols, own_sem, front_sem, send_sem, recv_sem
):
    half_ring = n // 2
    piece = depth // (2 * pieces)
    me = lax.axis_index("row")
    a, b = me // 2, me % 2
    spot = a + b * (n - 1 - 2 * a)

    def owner(place):
        place = (place + 2 * n) % n
        q = place // half_ring
        return 2 * (place + q * (n - 1 - 2 * place)) + q

    targets = (owner(spot + 1), owner(spot - 1))

    barrier = pltpu.get_barrier_semaphore()
    for target in targets:
        pl.semaphore_signal(barrier, inc=1, device_id={"row": target}, device_id_type=MESH)
    pl.semaphore_wait(barrier, 2)

    def rows_of(way, p):
        return pl.ds((way * pieces + p) * piece, piece)

    def source(step, way):
        return owner(spot - step) if way == 0 else owner(spot + step)

    def send(src, block, step, way, p):
        pltpu.make_async_remote_copy(
            src_ref=src,
            dst_ref=held.at[block, rows_of(way, p)],
            send_sem=send_sem.at[step, way, p],
            recv_sem=recv_sem.at[step, way, p],
            device_id={"row": targets[way]},
            device_id_type=MESH,
        ).start()

    def arrival(step, way, p):
        block = source(step + 1, way)
        rows = held.at[block, rows_of(way, p)]
        return pltpu.make_async_remote_copy(
            src_ref=rows,
            dst_ref=rows,
            send_sem=send_sem.at[step, way, p],
            recv_sem=recv_sem.at[step, way, p],
            device_id={"row": targets[way]},
            device_id_type=MESH,
        )

    def front_copy(block, way, p, slot):
        start = pl.multiple_of(block * depth + (way * pieces + p) * piece, piece)
        return pltpu.make_async_copy(
            front_ref.at[:, pl.ds(start, piece)], cols.at[slot], front_sem.at[slot]
        )

    for p in range(pieces):
        for way in range(2):
            send(omega_ref.at[rows_of(way, p)], me, 0, way, p)
    own = pltpu.make_async_copy(omega_ref, held.at[me], own_sem)
    own.start()
    for way in range(2):
        front_copy(me, way, 0, way).start()
    out_ref[...] = jnp.zeros_like(out_ref)
    own.wait()

    rows_tile = 256

    def multiply(block, way, p):
        @pl.loop(0, out_ref.shape[0] // rows_tile)
        def _(i):
            tile = pl.ds(pl.multiple_of(i * rows_tile, rows_tile), rows_tile)
            out_ref[tile, :] += jnp.dot(
                cols[way, tile, :],
                held[block, rows_of(way, p), :],
                precision=HIGHEST,
                preferred_element_type=jnp.float32,
            )

    def consume(step, p):
        for way in range(2):
            block = source(step, way)
            front_copy(block, way, p, way).wait()
            multiply(block, way, p)
            if p + 1 < pieces:
                front_copy(block, way, p + 1, way).start()
            else:

                @pl.when(step < n - 1)
                def _():
                    front_copy(source(step + 1, way), way, 0, way).start()

    for p in range(pieces):
        consume(0, p)

    @pl.loop(0, n - 1)
    def _(step):
        for p in range(pieces):
            for way in range(2):
                arrival(step, way, p).wait_recv()

                @pl.when(step < n - 2)
                def _():
                    block = source(step + 1, way)
                    send(held.at[block, rows_of(way, p)], block, step + 1, way, p)

            consume(step + 1, p)

    @pl.loop(0, n - 1)
    def _(step):
        for p in range(pieces):
            for way in range(2):
                arrival(step, way, p).wait_send()


def gather_matmul(front, omega, n):
    rows = front.shape[0]
    depth, width = omega.shape
    pieces = max(1, min(2, depth // 256))
    piece = depth // (2 * pieces)
    return pl.pallas_call(
        functools.partial(gather_matmul_kernel, n, depth, pieces),
        out_shape=jax.ShapeDtypeStruct((rows, width), jnp.float32),
        in_specs=[pl.BlockSpec(memory_space=pl.ANY)] * 2,
        out_specs=pl.BlockSpec(memory_space=pltpu.VMEM),
        scratch_shapes=[
            pltpu.VMEM((n, depth, width), jnp.float32),
            pltpu.VMEM((2, rows, piece), jnp.float32),
            pltpu.SemaphoreType.DMA,
            pltpu.SemaphoreType.DMA((2,)),
            pltpu.SemaphoreType.DMA((n - 1, 2, pieces)),
            pltpu.SemaphoreType.DMA((n - 1, 2, pieces)),
        ],
        compiler_params=pltpu.CompilerParams(
            collective_id=0, has_side_effects=True, vmem_limit_bytes=60 * 1024 * 1024
        ),
    )(front, omega)


def interpolate_kernel(problems, samples, merged, b2, b3, b4, s1, s2, s3, s4, *rest):
    leaf_out, *outs = rest[:5]
    inverse = rest[5]
    leaves = leaf_out.shape[0]
    block_rows, rank = leaf_out.shape[1:]
    pairs = []
    for leaf in range(leaves):
        pairs.append(
            (
                samples.at[pl.ds(leaf * block_rows, block_rows)],
                merged.at[pl.ds(leaf * rank, rank)],
                leaf_out.at[leaf],
            )
        )
    for block, chosen, out in zip((merged, b2, b3, b4), (s1, s2, s3, s4), outs):
        pairs.append((block, chosen, out.at[0]))

    def outer(x, y):
        return lax.dot_general(
            x, y, (((1,), (1,)), ((), ())), precision=HIGHEST, preferred_element_type=jnp.float32
        )

    lane = lax.broadcasted_iota(jnp.int32, (rank, rank), 1)
    sub = lax.broadcasted_iota(jnp.int32, (rank, rank), 0)
    for j, (block, chosen, out) in enumerate(pairs):
        gram = outer(chosen[...], chosen[...])
        inverse[j] = gram + jnp.where(lane == sub, ridge, 0.0)

    lane_row = lax.broadcasted_iota(jnp.int32, (1, rank), 1)

    @pl.loop(0, rank)
    def _(k):
        for j in range(len(pairs)):
            whole = inverse[j]
            row = inverse[j, pl.ds(k, 1), :]
            here = jnp.where(lane == k, whole, 0.0)
            column = jnp.sum(here, axis=1, keepdims=True)
            pivot = 1.0 / jnp.sum(jnp.where(lane_row == k, row, 0.0), axis=1, keepdims=True)
            scaled = jnp.where(lane_row == k, pivot, row * pivot)
            inverse[j] = jnp.where(lane == k, 0.0, whole) - column * scaled
            inverse[j, pl.ds(k, 1), :] = scaled

    for j, (block, chosen, out) in enumerate(pairs):
        cross = outer(block[...], chosen[...])
        out[...] = jnp.dot(
            cross, inverse[j], precision=HIGHEST, preferred_element_type=jnp.float32
        )


def partner(block, axis, apart):
    count = lax.axis_size(axis)
    route = []
    for low in range(count):
        high = low | 1 << apart
        if high != low and high < count:
            route += [(low, high), (high, low)]
    return lax.ppermute(block, axis, route)


def body(n, front, omega, leaf_pivots, pivots_one, pivots_two, pivots_three, pivots_four):
    rows_here = front.shape[0]
    width = omega.shape[1]
    samples = lax.psum(gather_matmul(front, omega, n), "col")
    leaf_count, rank = leaf_pivots.shape
    leaf_size = rows_here // leaf_count
    starts = leaf_size * jnp.arange(leaf_count, dtype=jnp.int32)[:, None]
    merged = jnp.take(samples, (leaf_pivots + starts).reshape(-1), axis=0)
    skeleton = jnp.take(merged, pivots_one[0], axis=0)
    skeletons = [skeleton]
    blocks = []
    position = lax.axis_index("row")
    for level, pivots in enumerate((pivots_two, pivots_three, pivots_four)):
        other = partner(skeleton, "row", level)
        lower = position >> level & 1 == 0
        block = jnp.where(
            lower, jnp.concatenate([skeleton, other], 0), jnp.concatenate([other, skeleton], 0)
        )
        node = position >> level + 1
        chosen_pivots = lax.dynamic_index_in_dim(pivots, node, 0, keepdims=False)
        skeleton = jnp.take(block, chosen_pivots, axis=0)
        blocks.append(block)
        skeletons.append(skeleton)
    problems = leaf_count + len(skeletons)
    basis = jax.ShapeDtypeStruct((1, leaf_size, rank), jnp.float32)
    outs = pl.pallas_call(
        functools.partial(interpolate_kernel, problems),
        out_shape=[jax.ShapeDtypeStruct((leaf_count, leaf_size, rank), jnp.float32)]
        + [basis] * len(skeletons),
        in_specs=[pl.BlockSpec(memory_space=pltpu.VMEM)] * 9,
        out_specs=[pl.BlockSpec(memory_space=pltpu.VMEM)] * 5,
        scratch_shapes=[pltpu.VMEM((problems, rank, rank), jnp.float32)],
    )(samples, merged, *blocks, *skeletons)
    return (samples, *outs)


def solution(mesh):
    in_specs = (
        P("row", "col"),
        P(("col", "row"), None),
        P("row", None),
        P("row", None),
        P(),
        P(),
        P(),
    )
    out_specs = (
        P("row", None),
        P("row", None, None),
        P("row", None, None),
        P("row", None, None),
        P("row", None, None),
        P("row", None, None),
    )
    return jax.shard_map(
        functools.partial(body, mesh.shape["row"]),
        mesh=mesh,
        in_specs=in_specs,
        out_specs=out_specs,
        check_vma=False,
    )
```

time: 1110 us -> 588 us (0.53)
  waiting for transfers between devices: 833 us -> 65.8 us
  Pallas kernels: 0 us -> 492 us
  other arithmetic: 144 us -> 2.18 us
  matrix products: 100 us -> 0 us
    all_gather x1 -> x0, waiting for transfers between devices: 794 us -> none  [body(): lax.all_gather(omega, 'row', axis=0, tiled=True)]
    pallas_call x0 -> x2, Pallas kernels: none -> 492 us  [the longest x1 406 us: gather_matmul(): pl.pallas_call(functools.partial(gather_matmul_kernel, n, depth, pieces),...]
    another operation x27 -> x0, other arithmetic: 137 us -> none  [the longest x16 73.6 us: interpolate(): factor = jnp.linalg.cholesky(gram)]
    dot_general x11 -> x0, matrix products: 96.4 us -> none  [the longest x1 87.6 us: body(): jnp.dot(front, lax.all_gather(omega, 'row', axis=0, tiled=True), precisio...]
    ppermute x3, waiting for transfers between devices: 0.01 us -> 27.1 us  [partner(): return lax.ppermute(block, axis, route)]
  transfers between devices with their start and end apart: 5 -> 4, of which waited for: 2 -> 4; matrix products, arithmetic and copies ran while one was open for 12% -> 0% of each run, Pallas kernels for 0% -> 0%
where the time goes in v1:
time: 588 us
  Pallas kernels  492 us (84%)
  waiting for transfers between devices  65.8 us (11%)
  between operations  14.3 us (2%)
  local copies, waits for them, and re-layouts  7.59 us (1%)
    pallas_call x1, Pallas kernels, gather_matmul(): pl.pallas_call(functools.partial(gather_matmul_kernel, n, depth, pieces),...  406 us
    pallas_call x1, Pallas kernels, body(): pl.pallas_call(functools.partial(interpolate_kernel, problems), out_shape...  86.3 us
    psum x1, waiting for transfers between devices, body(): samples = lax.psum(gather_matmul(front, omega, n), 'col')  38.6 us
    ppermute x3, waiting for transfers between devices, partner(): return lax.ppermute(block, axis, route)  27.1 us
  transfers between devices with their start and end apart: 4, of which 4 were waited for; matrix products, arithmetic and copies ran while one was open for 0% of the time, Pallas kernels for 0%

profile of v1, /device:TPU:0, one launch (start us, length us, event | category | flops | bytes accessed | tf_op | source)
XLA Modules:
  0.0 587.9 jit_solution(8034665097522038523)
XLA Ops:
  7.2 0.0 all-reduce.2.cloned.1.call-start
  7.2 406.1 %shard_map.118 = f32[512,640]{1,0:T(8,128)} custom-call(f32[512,16384]{1,0:T(8,128)} %front_ref.1, f32[2048,640]{1,0:T(8,128)} %omega_ref.1), custom_call_target="tpu_custom_call" | custom-call | tf_op jit(solution)/shard_map/pallas_call | solution.py:134
  413.4 0.0 copy-start.8
  413.4 0.0 copy-start.10
  413.4 0.0 all-reduce.2.cloned.1.call-update
  413.4 0.6 copy-done.8
  414.0 0.1 compare_and_fusion.4
  414.2 38.6 %all-reduce.2.cloned.1.call-done.samples = f32[512,640]{1,0:T(8,128)} async-done(((f32[512,640]{1,0:T(8,128)}), f32[512,640]{1,0:T(8,128)}) %all-reduce.2.cloned.1.call-update) | async-done | bytes 1310736 | tf_op jit(solution)/shard_map/psum | solution.py:215
  452.8 2.6 gather_fusion
  455.4 0.1 broadcast_select_fusion.merged
  455.5 0.0 copy-start.1
  455.5 0.0 copy-start.9
  455.6 0.8 gather_fusion.1
  456.4 0.1 broadcast_select_fusion.4.s1
  456.5 0.0 copy-start.5
  456.5 1.5 collective-permute-start
  458.0 0.7 compare_and_fusion.2
  458.8 7.1 %collective-permute-done = f32[128,640]{1,0:T(8,128)S(1)} collective-permute-done((f32[128,640]{1,0:T(8,128)S(1)}, f32[128,640]{1,0:T(8,128)S(1)}, u32[]{:S(2)}, u32[]{:S(2)}) %collective-permute-start) | collective-permute-done | bytes 327712 | tf_op jit(solution)/shard_map/ppermute | solution.py:209
  465.9 0.0 copy-start.11
  465.9 0.8 gather_fusion.2
  466.8 0.1 broadcast_select_fusion.3.s2
  466.9 1.6 collective-permute-start.1
  468.5 6.9 %collective-permute-done.1 = f32[128,640]{1,0:T(8,128)S(1)} collective-permute-done((f32[128,640]{1,0:T(8,128)S(1)}, f32[128,640]{1,0:T(8,128)S(1)}, u32[]{:S(2)}, u32[]{:S(2)}) %collective-permute-start.1) | collective-permute-done | bytes 327712 | tf_op jit(solution)/shard_map/ppermute | solution.py:209
  475.5 0.8 gather_fusion.3
  476.3 0.0 copy-done.3
  476.3 0.1 broadcast_select_fusion.2.s3
  476.4 2.5 collective-permute-start.2
  478.9 13.1 %collective-permute-done.2 = f32[128,640]{1,0:T(8,128)S(1)} collective-permute-done((f32[128,640]{1,0:T(8,128)S(1)}, f32[128,640]{1,0:T(8,128)S(1)}, u32[]{:S(2)}, u32[]{:S(2)}) %collective-permute-start.2) | collective-permute-done | bytes 327712 | tf_op jit(solution)/shard_map/ppermute | solution.py:209
  492.1 0.8 gather_fusion.4
  492.9 0.8 broadcast_select_fusion.1.s4
  493.7 86.3 %shard_map.119 = (f32[2,256,128]{2,1,0:T(8,128)}, f32[1,256,128]{2,1,0:T(8,128)}, f32[1,256,128]{2,1,0:T(8,128)}, f32[1,256,128]{2,1,0:T(8,128)}, f32[1,256,128]{2,1,0:T(8,128)}) custom-call(f32[512,640]{1,0:T(8,128)} %all-reduce.2.cloned.1.call-done.samples, f32[256,640]{1,0:T(8,128)} %copy-done.1, f32[256,640]{1,0:T(8,128)} %copy-done.2, ...), custom_call_target="tpu_custom_call" | custom-call | tf_op jit(solution)/shard_map/pallas_call | solution.py:237
  580.0 1.1 copy.15
  (31 shorter events, 0.2 us)
Async XLA Ops:
  7.2 445.6 %all-reduce.2.cloned.1.call-start = ((), (), s32[]{:S(2)}) async-start(), calls=%async_computation | async-start | bytes 2621440 | tf_op jit(solution)/shard_map/psum | solution.py:215
  413.4 0.7 copy-start.8
  413.4 0.8 copy-start.10
  455.5 0.8 copy-start.1
  455.5 3.2 copy-start.9
  456.5 10.3 %copy-start.5 = (f32[128,640]{1,0:T(8,128)}, f32[128,640]{1,0:T(8,128)S(1)}, u32[]{:S(2)}) copy-start(f32[128,640]{1,0:T(8,128)S(1)} %broadcast_select_fusion.4.s1) | copy-start | bytes 983044
  456.5 9.4 %collective-permute-start = (f32[128,640]{1,0:T(8,128)S(1)}, f32[128,640]{1,0:T(8,128)S(1)}, u32[]{:S(2)}, u32[]{:S(2)}) collective-permute-start(f32[128,640]{1,0:T(8,128)S(1)} %broadcast_select_fusion.4.s1), channel_id=1, source_target_pairs={{0,4},{4,0},{8,12},{12,8},{16,20},{20,16},{24,28},{28,24},{1,5},{5... | collective-permute-start | bytes 983048 | tf_op jit(solution)/shard_map/ppermute | solution.py:209
  465.9 0.9 copy-start.2
  465.9 2.5 copy-start.11
  466.9 9.4 %copy-start.6 = (f32[128,640]{1,0:T(8,128)}, f32[128,640]{1,0:T(8,128)S(1)}, u32[]{:S(2)}) copy-start(f32[128,640]{1,0:T(8,128)S(1)} %broadcast_select_fusion.3.s2) | copy-start | bytes 983044
  466.9 8.5 %collective-permute-start.1 = (f32[128,640]{1,0:T(8,128)S(1)}, f32[128,640]{1,0:T(8,128)S(1)}, u32[]{:S(2)}, u32[]{:S(2)}) collective-permute-start(f32[128,640]{1,0:T(8,128)S(1)} %broadcast_select_fusion.3.s2), channel_id=1, source_target_pairs={{0,8},{8,0},{4,12},{12,4},{16,24},{24,16},{20,28},{28,20},{1,9},{9... | collective-permute-start | bytes 983048 | tf_op jit(solution)/shard_map/ppermute | solution.py:209
  475.5 0.8 copy-start.3
  476.4 16.5 %copy-start.7 = (f32[128,640]{1,0:T(8,128)}, f32[128,640]{1,0:T(8,128)S(1)}, u32[]{:S(2)}) copy-start(f32[128,640]{1,0:T(8,128)S(1)} %broadcast_select_fusion.2.s3) | copy-start | bytes 983044
  476.4 15.6 %collective-permute-start.2 = (f32[128,640]{1,0:T(8,128)S(1)}, f32[128,640]{1,0:T(8,128)S(1)}, u32[]{:S(2)}, u32[]{:S(2)}) collective-permute-start(f32[128,640]{1,0:T(8,128)S(1)} %broadcast_select_fusion.2.s3), channel_id=1, source_target_pairs={{0,16},{16,0},{4,20},{20,4},{8,24},{24,8},{12,28},{28,12},{1,17},{... | collective-permute-start | bytes 983048 | tf_op jit(solution)/shard_map/ppermute | solution.py:209
  492.1 0.8 copy-start.4
  493.7 86.3 %copy-start = (f32[512,640]{1,0:T(8,128)S(1)}, f32[512,640]{1,0:T(8,128)}, u32[]{:S(2)}) copy-start(f32[512,640]{1,0:T(8,128)} %all-reduce.2.cloned.1.call-done.samples) | copy-start | bytes 3932164
Sparse Core Ops, SparseCore 0:
  413.5 39.2 all-reduce.1

commit v2 on v1

--- a/solution.py
+++ b/solution.py
@@ -13,7 +13,8 @@
 
 
 def gather_matmul_kernel(
-    n, depth, pieces, front_ref, omega_ref, out_ref, held, cols, own_sem, front_sem, send_sem, recv_sem
+    n, stages, depth, pieces, front_ref, omega_ref, out_ref, held, cols, total, landed, whole,
+    own_sem, front_sem, send_sem, recv_sem, sum_send, sum_recv
 ):
     half_ring = n // 2
     piece = depth // (2 * pieces)
@@ -27,11 +28,16 @@
         return 2 * (place + q * (n - 1 - 2 * place)) + q
 
     targets = (owner(spot + 1), owner(spot - 1))
+    lane = lax.axis_index("col")
+    sides = [(lane // (1 << t)) % 2 for t in range(stages)]
+    mates = [lane + (1 << t) * (1 - 2 * sides[t]) for t in range(stages)]
 
     barrier = pltpu.get_barrier_semaphore()
     for target in targets:
         pl.semaphore_signal(barrier, inc=1, device_id={"row": target}, device_id_type=MESH)
-    pl.semaphore_wait(barrier, 2)
+    for mate in mates:
+        pl.semaphore_signal(barrier, inc=1, device_id={"col": mate}, device_id_type=MESH)
+    pl.semaphore_wait(barrier, 2 + stages)
 
     def rows_of(way, p):
         return pl.ds((way * pieces + p) * piece, piece)
@@ -74,16 +80,16 @@
     own.start()
     for way in range(2):
         front_copy(me, way, 0, way).start()
-    out_ref[...] = jnp.zeros_like(out_ref)
+    total[...] = jnp.zeros_like(total)
     own.wait()
 
     rows_tile = 256
 
     def multiply(block, way, p):
-        @pl.loop(0, out_ref.shape[0] // rows_tile)
+        @pl.loop(0, total.shape[0] // rows_tile)
         def _(i):
             tile = pl.ds(pl.multiple_of(i * rows_tile, rows_tile), rows_tile)
-            out_ref[tile, :] += jnp.dot(
+            total[tile, :] += jnp.dot(
                 cols[way, tile, :],
                 held[block, rows_of(way, p), :],
                 precision=HIGHEST,
@@ -125,24 +131,70 @@
             for way in range(2):
                 arrival(step, way, p).wait_send()
 
-
-def gather_matmul(front, omega, n):
+    rows = total.shape[0]
+    base = 0
+    spans = []
+    for t in range(stages):
+        size = rows >> t + 1
+        keep = pl.multiple_of(base + sides[t] * size, 8)
+        give = pl.multiple_of(base + (1 - sides[t]) * size, 8)
+        spans.append((keep, size))
+        slot = landed.at[pl.ds(rows - (rows >> t), size)]
+        copy = pltpu.make_async_remote_copy(
+            src_ref=total.at[pl.ds(give, size)],
+            dst_ref=slot,
+            send_sem=sum_send.at[t],
+            recv_sem=sum_recv.at[t],
+            device_id={"col": mates[t]},
+            device_id_type=MESH,
+        )
+        copy.start()
+        copy.wait()
+        total[pl.ds(keep, size), :] += slot[...]
+        base = keep
+    if stages:
+        keep, size = spans[-1]
+        whole[pl.ds(keep, size), :] = total[pl.ds(keep, size), :]
+    else:
+        whole[...] = total[...]
+    for t in reversed(range(stages)):
+        keep, size = spans[t]
+        mine = whole.at[pl.ds(keep, size)]
+        copy = pltpu.make_async_remote_copy(
+            src_ref=mine,
+            dst_ref=mine,
+            send_sem=sum_send.at[stages + t],
+            recv_sem=sum_recv.at[stages + t],
+            device_id={"col": mates[t]},
+            device_id_type=MESH,
+        )
+        copy.start()
+        copy.wait()
+    out_ref[...] = whole[...]
+
+
+def gather_matmul(front, omega, n, stages):
     rows = front.shape[0]
     depth, width = omega.shape
     pieces = max(1, min(2, depth // 256))
     piece = depth // (2 * pieces)
     return pl.pallas_call(
-        functools.partial(gather_matmul_kernel, n, depth, pieces),
+        functools.partial(gather_matmul_kernel, n, stages, depth, pieces),
         out_shape=jax.ShapeDtypeStruct((rows, width), jnp.float32),
         in_specs=[pl.BlockSpec(memory_space=pl.ANY)] * 2,
         out_specs=pl.BlockSpec(memory_space=pltpu.VMEM),
         scratch_shapes=[
             pltpu.VMEM((n, depth, width), jnp.float32),
             pltpu.VMEM((2, rows, piece), jnp.float32),
+            pltpu.VMEM((rows, width), jnp.float32),
+            pltpu.VMEM((rows, width), jnp.float32),
+            pltpu.VMEM((rows, width), jnp.float32),
             pltpu.SemaphoreType.DMA,
             pltpu.SemaphoreType.DMA((2,)),
             pltpu.SemaphoreType.DMA((n - 1, 2, pieces)),
             pltpu.SemaphoreType.DMA((n - 1, 2, pieces)),
+            pltpu.SemaphoreType.DMA((2 * stages,)),
+            pltpu.SemaphoreType.DMA((2 * stages,)),
         ],
         compiler_params=pltpu.CompilerParams(
             collective_id=0, has_side_effects=True, vmem_limit_bytes=60 * 1024 * 1024
@@ -150,22 +202,9 @@
     )(front, omega)
 
 
-def interpolate_kernel(problems, samples, merged, b2, b3, b4, s1, s2, s3, s4, *rest):
-    leaf_out, *outs = rest[:5]
-    inverse = rest[5]
-    leaves = leaf_out.shape[0]
-    block_rows, rank = leaf_out.shape[1:]
-    pairs = []
-    for leaf in range(leaves):
-        pairs.append(
-            (
-                samples.at[pl.ds(leaf * block_rows, block_rows)],
-                merged.at[pl.ds(leaf * rank, rank)],
-                leaf_out.at[leaf],
-            )
-        )
-    for block, chosen, out in zip((merged, b2, b3, b4), (s1, s2, s3, s4), outs):
-        pairs.append((block, chosen, out.at[0]))
+def interpolate_kernel(count, *refs):
+    blocks, chosens, outs, inverses = [refs[i * count : (i + 1) * count] for i in range(4)]
+    rank = outs[0].shape[2]
 
     def outer(x, y):
         return lax.dot_general(
@@ -174,29 +213,61 @@
 
     lane = lax.broadcasted_iota(jnp.int32, (rank, rank), 1)
     sub = lax.broadcasted_iota(jnp.int32, (rank, rank), 0)
-    for j, (block, chosen, out) in enumerate(pairs):
-        gram = outer(chosen[...], chosen[...])
-        inverse[j] = gram + jnp.where(lane == sub, ridge, 0.0)
-
     lane_row = lax.broadcasted_iota(jnp.int32, (1, rank), 1)
-
-    @pl.loop(0, rank)
-    def _(k):
-        for j in range(len(pairs)):
-            whole = inverse[j]
-            row = inverse[j, pl.ds(k, 1), :]
-            here = jnp.where(lane == k, whole, 0.0)
-            column = jnp.sum(here, axis=1, keepdims=True)
-            pivot = 1.0 / jnp.sum(jnp.where(lane_row == k, row, 0.0), axis=1, keepdims=True)
-            scaled = jnp.where(lane_row == k, pivot, row * pivot)
-            inverse[j] = jnp.where(lane == k, 0.0, whole) - column * scaled
-            inverse[j, pl.ds(k, 1), :] = scaled
-
-    for j, (block, chosen, out) in enumerate(pairs):
+    for chosen, inverse in zip(chosens, inverses):
+        inverse[...] = outer(chosen[...], chosen[...]) + jnp.where(lane == sub, ridge, 0.0)
+
+    def pick(values, at, index):
+        return jnp.sum(jnp.where(at == index, values, 0.0), axis=1, keepdims=True)
+
+    @pl.loop(0, rank // 2)
+    def _(step):
+        k = 2 * step
+        wholes = [inverse[...] for inverse in inverses]
+        firsts = [inverse[pl.ds(k, 1), :] for inverse in inverses]
+        seconds = [inverse[pl.ds(k + 1, 1), :] for inverse in inverses]
+        corners = [
+            (pick(u, lane_row, k), pick(u, lane_row, k + 1), pick(v, lane_row, k), pick(v, lane_row, k + 1))
+            for u, v in zip(firsts, seconds)
+        ]
+        lefts = [pick(whole, lane, k) for whole in wholes]
+        rights = [pick(whole, lane, k + 1) for whole in wholes]
+        news = []
+        for (a, b, c, d), u, v in zip(corners, firsts, seconds):
+            top = 1.0 / a
+            beta = b * top
+            s = jnp.where(lane_row == k, top, u * top)
+            v1 = jnp.where(lane_row == k, 0.0, v) - c * s
+            low = 1.0 / (d - c * beta)
+            t = jnp.where(lane_row == k + 1, low, v1 * low)
+            w = jnp.where(lane_row == k + 1, 0.0, s) - beta * t
+            news.append((w, t))
+        for inverse, whole, p, q, (w, t) in zip(inverses, wholes, lefts, rights, news):
+            rest = jnp.where(lane // 2 == step, 0.0, whole) - p * w - q * t
+            inverse[...] = jnp.where(sub == k, w, jnp.where(sub == k + 1, t, rest))
+
+    for block, chosen, out, inverse in zip(blocks, chosens, outs, inverses):
         cross = outer(block[...], chosen[...])
-        out[...] = jnp.dot(
-            cross, inverse[j], precision=HIGHEST, preferred_element_type=jnp.float32
-        )
+        out[0] = jnp.dot(
+            cross, inverse[...], precision=HIGHEST, preferred_element_type=jnp.float32
+        )
+
+
+def interpolate(blocks, chosens):
+    count = len(blocks)
+    leaf_size, width = blocks[0].shape
+    rank = chosens[0].shape[0]
+    basis = jax.ShapeDtypeStruct((1, leaf_size, rank), jnp.float32)
+    return pl.pallas_call(
+        functools.partial(interpolate_kernel, count),
+        out_shape=[basis] * count,
+        in_specs=[pl.BlockSpec(memory_space=pltpu.VMEM)] * (2 * count),
+        out_specs=[pl.BlockSpec(memory_space=pltpu.VMEM)] * count,
+        scratch_shapes=[pltpu.VMEM((rank, rank), jnp.float32)] * count,
+        cost_estimate=pl.CostEstimate(
+            flops=10**10, bytes_accessed=4 * count * (leaf_size + rank) * width, transcendentals=0
+        ),
+    )(*blocks, *chosens)
 
 
 def partner(block, axis, apart):
@@ -209,10 +280,10 @@
     return lax.ppermute(block, axis, route)
 
 
-def body(n, front, omega, leaf_pivots, pivots_one, pivots_two, pivots_three, pivots_four):
+def body(n, stages, front, omega, leaf_pivots, pivots_one, pivots_two, pivots_three, pivots_four):
     rows_here = front.shape[0]
     width = omega.shape[1]
-    samples = lax.psum(gather_matmul(front, omega, n), "col")
+    samples = gather_matmul(front, omega, n, stages)
     leaf_count, rank = leaf_pivots.shape
     leaf_size = rows_here // leaf_count
     starts = leaf_size * jnp.arange(leaf_count, dtype=jnp.int32)[:, None]
@@ -232,17 +303,11 @@
         skeleton = jnp.take(block, chosen_pivots, axis=0)
         blocks.append(block)
         skeletons.append(skeleton)
-    problems = leaf_count + len(skeletons)
-    basis = jax.ShapeDtypeStruct((1, leaf_size, rank), jnp.float32)
-    outs = pl.pallas_call(
-        functools.partial(interpolate_kernel, problems),
-        out_shape=[jax.ShapeDtypeStruct((leaf_count, leaf_size, rank), jnp.float32)]
-        + [basis] * len(skeletons),
-        in_specs=[pl.BlockSpec(memory_space=pltpu.VMEM)] * 9,
-        out_specs=[pl.BlockSpec(memory_space=pltpu.VMEM)] * 5,
-        scratch_shapes=[pltpu.VMEM((problems, rank, rank), jnp.float32)],
-    )(samples, merged, *blocks, *skeletons)
-    return (samples, *outs)
+    leaves = [samples[i * leaf_size : (i + 1) * leaf_size] for i in range(leaf_count)]
+    chosens = [merged[i * rank : (i + 1) * rank] for i in range(leaf_count)]
+    *leaf_basis, basis_one = interpolate(leaves + [merged], chosens + skeletons[:1])
+    upper = interpolate(blocks, skeletons[1:])
+    return (samples, jnp.concatenate(leaf_basis), basis_one, *upper)
 
 
 def solution(mesh):
@@ -264,7 +329,7 @@
         P("row", None, None),
     )
     return jax.shard_map(
-        functools.partial(body, mesh.shape["row"]),
+        functools.partial(body, mesh.shape["row"], (mesh.shape["col"] - 1).bit_length()),
         mesh=mesh,
         in_specs=in_specs,
         out_specs=out_specs,

time: 588 us -> 513 us (0.87)
  waiting for transfers between devices: 65.8 us -> 22.4 us
  Pallas kernels: 492 us -> 468 us
  between operations: 14.3 us -> 0.85 us
    psum x1 -> x0, waiting for transfers between devices: 38.6 us -> none  [body(): samples = lax.psum(gather_matmul(front, omega, n), 'col')]
    pallas_call x2 -> x3, Pallas kernels: 492 us -> 468 us  [the longest x1 428 us: gather_matmul(): pl.pallas_call(functools.partial(gather_matmul_kernel, n, stages, depth,...]
  transfers between devices with their start and end apart: 4 -> 3, of which waited for: 4 -> 2; matrix products, arithmetic and copies ran while one was open for 0% -> 1% of each run, Pallas kernels for 0% -> 4%
where the time goes in v2:
time: 513 us
  Pallas kernels  468 us (91%)
  waiting for transfers between devices  22.4 us (4%)
  other arithmetic  8.01 us (2%)
  local copies, waits for them, and re-layouts  7.98 us (2%)
  starting transfers between devices  5.81 us (1%)
    pallas_call x1, Pallas kernels, gather_matmul(): pl.pallas_call(functools.partial(gather_matmul_kernel, n, stages, depth,...  428 us
    pallas_call x2, Pallas kernels, interpolate(): pl.pallas_call(functools.partial(interpolate_kernel, count), out_shape=[b...  40 us
    ppermute x3, waiting for transfers between devices, partner(): return lax.ppermute(block, axis, route)  22.4 us
  transfers between devices with their start and end apart: 3, of which 2 were waited for; matrix products, arithmetic and copies ran while one was open for 1% of the time, Pallas kernels for 4%

profile of v2, /device:TPU:0, one launch (start us, length us, event | category | flops | bytes accessed | tf_op | source)
XLA Modules:
  0.0 512.9 jit_solution(5756344119202111064)
XLA Ops:
  0.6 0.7 compare_select_fusion.5
  1.3 0.7 compare_and_fusion.3
  2.0 0.8 compare_and_fusion.4
  2.7 427.8 %shard_map.118 = f32[512,640]{1,0:T(8,128)} custom-call(f32[512,16384]{1,0:T(8,128)} %front_ref.1, f32[2048,640]{1,0:T(8,128)} %omega_ref.1), custom_call_target="tpu_custom_call" | custom-call | tf_op jit(solution)/shard_map/pallas_call | solution.py:181
  430.6 2.7 gather_fusion
  433.3 1.2 fusion
  434.5 0.8 gather_fusion.1
  435.3 0.1 broadcast_select_fusion.4.refs_5_
  435.4 1.6 collective-permute-start
  437.0 0.9 fusion.1
  437.9 0.7 compare_and_fusion.2
  438.6 0.0 copy-start.8
  438.6 20.0 %shard_map.119 = (f32[1,256,128]{2,1,0:T(8,128)}, f32[1,256,128]{2,1,0:T(8,128)}, f32[1,256,128]{2,1,0:T(8,128)}) custom-call(f32[256,640]{1,0:T(8,128)} %get-tuple-element.26.refs_0_, f32[256,640]{1,0:T(8,128)} %get-tuple-element.25.refs_1_, f32[256,640]{1,0:T(8,128)} %copy-done.1, f32[128,640]{1,0:T(8,128)} %get-tuple-element.28.refs_3_, ...), custom_call_target="tpu_custom_call" | custom-call | flops 10000000000 | bytes 2949120 | tf_op jit(solution)/shard_map/pallas_call | solution.py:261
  458.7 1.7 pad_maximum_fusion
  460.3 0.0 collective-permute-done
  460.4 1.1 maximum_select_fusion.refs_0_
  461.5 0.0 copy-start.2
  461.5 0.0 copy-start.9
  461.5 0.8 gather_fusion.2
  462.3 0.1 broadcast_select_fusion.3.refs_3_
  462.4 1.6 collective-permute-start.1
  464.1 8.1 %collective-permute-done.1 = f32[128,640]{1,0:T(8,128)S(1)} collective-permute-done((f32[128,640]{1,0:T(8,128)S(1)}, f32[128,640]{1,0:T(8,128)S(1)}, u32[]{:S(2)}, u32[]{:S(2)}) %collective-permute-start.1) | collective-permute-done | bytes 327712 | tf_op jit(solution)/shard_map/ppermute | solution.py:280
  472.3 0.8 gather_fusion.3
  473.1 0.0 copy-done.3
  473.1 0.1 broadcast_select_fusion.2.refs_4_
  473.2 2.6 collective-permute-start.2
  475.8 14.2 %collective-permute-done.2 = f32[128,640]{1,0:T(8,128)S(1)} collective-permute-done((f32[128,640]{1,0:T(8,128)S(1)}, f32[128,640]{1,0:T(8,128)S(1)}, u32[]{:S(2)}, u32[]{:S(2)}) %collective-permute-start.2) | collective-permute-done | bytes 327712 | tf_op jit(solution)/shard_map/ppermute | solution.py:280
  490.1 0.8 gather_fusion.4
  491.0 0.0 copy-done.4
  491.0 0.8 broadcast_select_fusion.1.refs_5_
  491.8 20.0 %shard_map.120 = (f32[1,256,128]{2,1,0:T(8,128)}, f32[1,256,128]{2,1,0:T(8,128)}, f32[1,256,128]{2,1,0:T(8,128)}) custom-call(f32[256,640]{1,0:T(8,128)} %copy-done.2, f32[256,640]{1,0:T(8,128)} %copy-done.3, f32[256,640]{1,0:T(8,128)} %copy-done.4, f32[128,640]{1,0:T(8,128)} %copy-done.6, f32[128,640]{1,0:T(8,128)} %copy-done.7, ...), custom_call_target="tpu_custom_call" | custom-call | flops 10000000000 | bytes 2949120 | tf_op jit(solution)/shard_map/pallas_call | solution.py:261
  511.8 1.1 copy.14
  (27 shorter events, 0.2 us)
Async XLA Ops:
  430.6 2.7 copy-start
  434.5 2.5 copy-start.1
  435.4 3.2 copy-start.5
  435.4 24.9 %collective-permute-start = (f32[128,640]{1,0:T(8,128)S(1)}, f32[128,640]{1,0:T(8,128)S(1)}, u32[]{:S(2)}, u32[]{:S(2)}) collective-permute-start(f32[128,640]{1,0:T(8,128)S(1)} %broadcast_select_fusion.4.refs_5_), channel_id=1, source_target_pairs={{0,4},{4,0},{8,12},{12,8},{16,20},{20,16},{24,28},{28,24},{1,5},{5... | collective-permute-start | bytes 983048 | tf_op jit(solution)/shard_map/ppermute | solution.py:280
  438.6 20.0 %copy-start.8 = (s32[2,128]{1,0:T(2,128)S(1)}, s32[2,128]{1,0:T(2,128)}, u32[]{:S(2)}) copy-start(s32[2,128]{1,0:T(2,128)} %param.14) | copy-start | bytes 3076
  461.5 0.8 copy-start.2
  461.5 2.6 copy-start.9
  462.4 10.7 %copy-start.6 = (f32[128,640]{1,0:T(8,128)}, f32[128,640]{1,0:T(8,128)S(1)}, u32[]{:S(2)}) copy-start(f32[128,640]{1,0:T(8,128)S(1)} %broadcast_select_fusion.3.refs_3_) | copy-start | bytes 983044
  462.4 9.8 %collective-permute-start.1 = (f32[128,640]{1,0:T(8,128)S(1)}, f32[128,640]{1,0:T(8,128)S(1)}, u32[]{:S(2)}, u32[]{:S(2)}) collective-permute-start(f32[128,640]{1,0:T(8,128)S(1)} %broadcast_select_fusion.3.refs_3_), channel_id=1, source_target_pairs={{0,8},{8,0},{4,12},{12,4},{16,24},{24,16},{20,28},{28,20},{1,9},{9... | collective-permute-start | bytes 983048 | tf_op jit(solution)/shard_map/ppermute | solution.py:280
  472.3 0.9 copy-start.3
  473.2 17.7 %copy-start.7 = (f32[128,640]{1,0:T(8,128)}, f32[128,640]{1,0:T(8,128)S(1)}, u32[]{:S(2)}) copy-start(f32[128,640]{1,0:T(8,128)S(1)} %broadcast_select_fusion.2.refs_4_) | copy-start | bytes 983044
  473.2 16.8 %collective-permute-start.2 = (f32[128,640]{1,0:T(8,128)S(1)}, f32[128,640]{1,0:T(8,128)S(1)}, u32[]{:S(2)}, u32[]{:S(2)}) collective-permute-start(f32[128,640]{1,0:T(8,128)S(1)} %broadcast_select_fusion.2.refs_4_), channel_id=1, source_target_pairs={{0,16},{16,0},{4,20},{20,4},{8,24},{24,8},{12,28},{28,12},{1,17},{... | collective-permute-start | bytes 983048 | tf_op jit(solution)/shard_map/ppermute | solution.py:280
  490.1 0.8 copy-start.4
